TPU v7x, 32 devices: a whole 2x2x4 slice. The times are simulated.
32 devices in a mesh: seq: 16 (over z, x, core), head: 2 (over y).
Axes of the slice: x: 2, y: 2, z: 4, core: 2. Of those that a mesh axis runs over, the one named last changes fastest.
Arguments:
- hidden: bfloat16 [4608, 8192], P('seq'), may hold values from -6 to 6
- norm_gain: bfloat16 [8192], replicated, may hold values from 0.099609375 to 1.8984375
- w_query: bfloat16 [8192, 1024], P('seq', 'head'), may hold values from -0.125 to 0.125
- w_key: bfloat16 [8192, 256], P('seq', 'head'), may hold values from -0.125 to 0.125
- w_value: bfloat16 [8192, 256], P('seq', 'head'), may hold values from -0.0625 to 0.0625
- bias_query: bfloat16 [1024], P('head'), may hold values from -3 to 3
- bias_key: bfloat16 [256], P('head'), may hold values from -200 to 200
- bias_value: bfloat16 [256], P('head'), may hold values from -3 to 3
- w_out: bfloat16 [1024, 8192], P('head', 'seq'), may hold values from -0.1875 to 0.1875
Outputs:
- attn_out: bfloat16 [4608, 8192], P(('seq', 'head'))
All inputs are finite; a program needn't handle non-finite values.
Results may differ from a plain program's by a relative error of at most 0.014.
The roundings to bfloat16 on the way count: a program that leaves them out, or rounds other values in their place, can miss the bound.
Values may be sent and summed in bfloat16 or wider, within the bound.
No kernel may reach another device: no remote copies, remote signals or barrier semaphores. Data moves between devices by JAX's collectives and lax.ppermute only.
A program may use at most 192 MiB of HBM per device.

v0:
```python
import jax
import jax.numpy as jnp
from jax import lax
from jax.sharding import PartitionSpec as P

HEAD_DIM = 128
ROPE_BASE = 1000000.0
EPSILON = 1e-06


def rotary(values, positions):
    half_dim = values.shape[-1] // 2
    freq = ROPE_BASE ** (-2.0 * jnp.arange(half_dim, dtype=jnp.float32) / values.shape[-1])
    angles = positions.astype(jnp.float32)[:, None, None] * freq[None, None, :]
    cosine = jnp.cos(angles)
    sine = jnp.sin(angles)
    first = values[..., :half_dim]
    second = values[..., half_dim:]
    return jnp.concatenate(
        [first * cosine - second * sine, second * cosine + first * sine], axis=-1
    )


def local(hidden, norm_gain, w_query, w_key, w_value, bias_query, bias_key, bias_value, w_out):
    row_count = hidden.shape[0]
    head_count = w_query.shape[1] // HEAD_DIM
    first_row = lax.axis_index("seq") * row_count
    last_row = first_row + row_count - 1
    positions = first_row + jnp.arange(row_count, dtype=jnp.int32)
    widened = hidden.astype(jnp.float32)
    inverse = lax.rsqrt(jnp.mean(widened * widened, axis=-1, keepdims=True) + EPSILON)
    normed = (widened * inverse * norm_gain.astype(jnp.float32)).astype(jnp.bfloat16)
    query = jnp.dot(
        normed,
        lax.all_gather(w_query, "seq", axis=0, tiled=True),
        preferred_element_type=jnp.float32,
    )
    keys = jnp.dot(
        normed, lax.all_gather(w_key, "seq", axis=0, tiled=True), preferred_element_type=jnp.float32
    )
    values = jnp.dot(
        normed,
        lax.all_gather(w_value, "seq", axis=0, tiled=True),
        preferred_element_type=jnp.float32,
    )
    query = query + bias_query.astype(jnp.float32)
    keys = keys + bias_key.astype(jnp.float32)
    values = values + bias_value.astype(jnp.float32)
    query = rotary(query.reshape(row_count, head_count, HEAD_DIM), positions).astype(jnp.bfloat16)
    keys = (
        rotary(keys.reshape(row_count, 1, HEAD_DIM), positions)
        .reshape(row_count, HEAD_DIM)
        .astype(jnp.bfloat16)
    )
    values = values.astype(jnp.bfloat16)
    query_heads = query.transpose(1, 0, 2)
    scaling = HEAD_DIM ** (-0.5)
    initial = (
        jnp.full((head_count, row_count), -1e30, jnp.float32),
        jnp.zeros((head_count, row_count), jnp.float32),
        jnp.zeros((head_count, row_count, HEAD_DIM), jnp.float32),
    )
    key_piece = lax.all_gather(keys, "seq", axis=0, tiled=True)
    value_piece = lax.all_gather(values, "seq", axis=0, tiled=True)

    def update(state):
        highest, total, summed = state
        scores = (
            jnp.einsum("hqd,kd->hqk", query_heads, key_piece, preferred_element_type=jnp.float32)
            * scaling
        )
        key_positions = jnp.arange(key_piece.shape[0], dtype=jnp.int32)
        allowed = positions[:, None] >= key_positions[None, :]
        scores = jnp.where(allowed[None], scores, -jnp.inf)
        new_high = jnp.maximum(highest, jnp.max(scores, axis=-1))
        probs = jnp.exp(scores - new_high[..., None])
        total = jnp.sum(probs, axis=-1)
        mixed = jnp.einsum(
            "hqk,kd->hqd",
            probs.astype(jnp.bfloat16),
            value_piece,
            preferred_element_type=jnp.float32,
        )
        return (new_high, total, mixed)

    def unchanged(state):
        return state

    highest, total, summed = lax.cond(jnp.int32(0) <= last_row, update, unchanged, initial)
    attended = (summed / total[..., None]).astype(jnp.bfloat16)
    attended = attended.transpose(1, 0, 2).reshape(row_count, head_count * HEAD_DIM)
    partial_out = jnp.dot(
        attended,
        lax.all_gather(w_out, "seq", axis=1, tiled=True),
        preferred_element_type=jnp.float32,
    )
    result = lax.psum_scatter(
        partial_out.astype(jnp.bfloat16), "head", scatter_dimension=0, tiled=True
    )
    return result


def solution(mesh):
    in_specs = (
        P("seq", None),
        P(),
        P("seq", "head"),
        P("seq", "head"),
        P("seq", "head"),
        P("head"),
        P("head"),
        P("head"),
        P("head", "seq"),
    )
    out_specs = P(("seq", "head"), None)
    return jax.shard_map(local, mesh=mesh, in_specs=in_specs, out_specs=out_specs, check_vma=False)
```

profile of v0, /device:TPU:0, one launch (start us, length us, event | category | flops | bytes accessed | tf_op | source)
XLA Modules:
  0.0 401.3 jit_solution(17232137514900571910)
XLA Ops:
  6.5 0.0 all-gather.10.cloned.1.call-start
  6.5 0.7 all-gather.10.cloned.1.call-update
  7.3 0.0 all-gather.12.cloned.1.call-start
  7.3 0.7 all-gather.12.cloned.1.call-update
  8.0 0.0 all-gather.8.cloned.1.call-start
  8.1 0.7 all-gather.8.cloned.1.call-update
  8.7 0.0 all-gather.18.cloned.1.call-start
  8.8 0.7 convert_element_type.48
  9.5 0.7 convert_element_type.52
  10.2 3.4 fusion.11
  13.5 0.0 copy-start.1
  13.6 40.1 %all-gather.10.cloned.1.call-done = bf16[8192,128]{1,0:T(8,128)(2,1)} async-done(((bf16[512,128]{1,0:T(8,128)(2,1)}), bf16[8192,128]{1,0:T(8,128)(2,1)}) %all-gather.10.cloned.1.call-update) | async-done | bytes 2097168 | tf_op jit(solution)/shard_map/all_gather | solution.py:39
  53.7 4.6 %fusion.14 = f32[288,1,128]{2,0,1:T(8,128)S(1)} fusion(bf16[8192,128]{1,0:T(8,128)(2,1)} %all-gather.10.cloned.1.call-done, f32[128]{0:T(128)S(1)} %convert_element_type.52, bf16[288,8192]{1,0:T(8,128)(2,1)} %param.11, f32[8192]{0:T(1024)S(1)} %convert_element_type.48, f32[288]{0:T(512)S(1)} %add_rsqrt_fusion), kind=kOutput, calls=%fused_computation.24 | convolution fusion | flops 613453824 | bytes 6997632 | tf_op jit(solution)/shard_map/dot_general | solution.py:38
  58.3 0.0 copy-start
  58.3 0.7 fusion.24
  58.9 0.7 pad_maximum_fusion
  59.7 0.0 all-gather.18.cloned.1.call-update
  59.7 0.0 all-gather.14.cloned.1.call-start
  59.7 0.0 copy-done.1
  59.8 36.3 %all-gather.12.cloned.1.call-done = bf16[8192,128]{1,0:T(8,128)(2,1)} async-done(((bf16[512,128]{1,0:T(8,128)(2,1)}), bf16[8192,128]{1,0:T(8,128)(2,1)}) %all-gather.12.cloned.1.call-update) | async-done | bytes 2097168 | tf_op jit(solution)/shard_map/all_gather | solution.py:43
  96.1 5.1 %fusion.15 = bf16[288,128]{1,0:T(8,128)(2,1)} fusion(bf16[8192,128]{1,0:T(8,128)(2,1)} %all-gather.12.cloned.1.call-done, f32[128]{0:T(128)S(1)} %convert_element_type.54, bf16[288,8192]{1,0:T(8,128)(2,1)} %param.11, f32[8192]{0:T(1024)S(1)} %convert_element_type.48, f32[288]{0:T(512)S(1)} %add_rsqrt_fusion), kind=kOutput, calls=%fused_computation.25 | convolution fusion | flops 613490688 | bytes 6923904 | tf_op jit(solution)/shard_map/dot_general | solution.py:41
  101.2 0.0 all-gather.14.cloned.1.call-update
  101.2 0.0 all-gather.16.cloned.1.call-start
  101.3 0.5 all-gather.16.cloned.1.call-update
  101.8 0.2 reduce-scatter.2.cloned.1.call-start
  102.0 0.0 copy-done
  102.1 0.6 multiply_cosine_fusion.1
  102.7 68.6 %all-gather.8.cloned.1.call-done = bf16[8192,512]{1,0:T(8,128)(2,1)} async-done(((bf16[512,512]{1,0:T(8,128)(2,1)}), bf16[8192,512]{1,0:T(8,128)(2,1)}) %all-gather.8.cloned.1.call-update) | async-done | bytes 8388624 | tf_op jit(solution)/shard_map/all_gather | solution.py:35
  171.3 7.0 %convolution_add_fusion = f32[288,512]{1,0:T(8,128)S(1)} fusion(bf16[8192,512]{1,0:T(8,128)(2,1)} %all-gather.8.cloned.1.call-done, f32[512]{0:T(512)S(1)} %convert_element_type.50, bf16[288,8192]{1,0:T(8,128)(2,1)} %param.11, f32[8192]{0:T(1024)S(1)} %convert_element_type.48, f32[288]{0:T(512)S(1)} %add_rsqrt_fusion), kind=kOutput, calls=%fused_computation.21 | convolution fusion | flops 2425503744 | bytes 13732992 | tf_op jit(solution)/shard_map/dot_general | solution.py:33
  178.3 0.2 reshape.159
  178.6 0.4 fusion.30
  178.9 0.2 subtract_convert_fusion
  179.1 0.2 maximum_bitcast_fusion
  179.3 31.1 %all-gather.18.cloned.1.call-done = bf16[4608,1,128]{2,0,1:T(8,128)(2,1)} async-done(((bf16[288,1,128]{2,0,1:T(8,128)(2,1)}), bf16[4608,1,128]{2,0,1:T(8,128)(2,1)}) %all-gather.18.cloned.1.call-update) | async-done | bytes 1179664 | tf_op jit(solution)/shard_map/all_gather | solution.py:63
  210.3 39.3 %all-gather.14.cloned.1.call-done = bf16[4608,128]{1,0:T(8,128)(2,1)} async-done(((bf16[288,128]{1,0:T(8,128)(2,1)}), bf16[4608,128]{1,0:T(8,128)(2,1)}) %all-gather.14.cloned.1.call-update) | async-done | bytes 1179664 | tf_op jit(solution)/shard_map/all_gather | solution.py:64
  249.7 19.5 %conditional.1 = (f32[4,288]{1,0:T(4,128)S(1)}, f32[4,288,128]{2,1,0:T(8,128)S(1)}) conditional(s32[]{:T(128)} %convert_element_type.46, () %tuple.13, (s32[]{:T(128)}, s32[288]{0:T(512)S(1)}, bf16[4,288,128]{2,1,0:T(8,128)(2,1)S(1)}, bf16[4608,128]{1,0:T(8,128)(2,1)}, bf16[4608,128]{1,0:T(8,128)(2,1)}) %tuple.36), branch_computations={%region_1.0_spmd, %region_2.5_spmd} | conditional | flops 2777627648 | bytes 72284560 | solution.py:89
  249.7 0.8 iota_compare_fusion
  250.5 5.5 %fusion = (f32[4,288]{1,0:T(4,128)S(1)}, f32[4,288,4608]{2,1,0:T(8,128)S(1)}) fusion(pred[288,4608]{1,0:T(8,128)(4,1)S(1)} %iota_compare_fusion, bf16[4,288,128]{2,1,0:T(8,128)(2,1)S(1)} %get-tuple-element.19, bf16[4608,128]{1,0:T(8,128)(2,1)} %get-tuple-element.20), kind=kOutput, calls=%fused_computation.2 | convolution fusion | flops 1374878592 | bytes 24039936 | tf_op jit(solution)/shard_map/cond/branch_1_fun/hqd,kd->hqk/dot_general | solution.py:69
  255.9 6.6 %fusion.3 = f32[4,288,128]{2,1,0:T(8,128)S(1)} fusion(f32[4,288,4608]{2,1,0:T(8,128)S(1)} %get-tuple-element.27, f32[4,288]{1,0:T(4,128)S(1)} %broadcast_maximum_fusion, pred[288,4608]{1,0:T(8,128)(4,1)S(1)} %iota_compare_fusion, bf16[4608,128]{1,0:T(8,128)(2,1)} %get-tuple-element.21), kind=kOutput, calls=%fused_computation.5 | convolution fusion | flops 1380188160 | bytes 24334848 | tf_op jit(solution)/shard_map/cond/branch_1_fun/hqk,kd->hqd/dot_general | solution.py:78
  262.6 6.6 %fusion.2 = f32[4,288]{1,0:T(4,128)S(1)} fusion(f32[4,288,4608]{2,1,0:T(8,128)S(1)} %get-tuple-element.27, f32[4,288]{1,0:T(4,128)S(1)} %broadcast_maximum_fusion, pred[288,4608]{1,0:T(8,128)(4,1)S(1)} %iota_compare_fusion), kind=kLoop, calls=%fused_computation.4 | loop fusion | flops 21232512 | bytes 22569984 | tf_op jit(solution)/shard_map/cond/branch_1_fun/reduce_sum | solution.py:77
  269.2 59.2 %all-gather.16.cloned.1.call-done = bf16[512,8192]{1,0:T(8,128)(2,1)} async-done(((bf16[512,512]{1,0:T(8,128)(2,1)}), bf16[512,8192]{1,0:T(8,128)(2,1)}) %all-gather.16.cloned.1.call-update) | async-done | bytes 8388624 | tf_op jit(solution)/shard_map/all_gather | solution.py:94
  328.3 7.7 %convolution_convert_fusion = bf16[288,8192]{1,0:T(8,128)(2,1)} fusion(bf16[512,8192]{1,0:T(8,128)(2,1)} %all-gather.16.cloned.1.call-done, f32[4,288,128]{2,1,0:T(8,128)S(1)} %get-tuple-element.24, f32[4,288]{1,0:T(4,128)S(1)} %get-tuple-element.25), kind=kOutput, calls=%fused_computation.17 | convolution fusion | flops 2418573312 | bytes 13701632 | tf_op jit(solution)/shard_map/dot_general | solution.py:92
  336.0 0.0 reduce-scatter.2.cloned.1.call-update
  336.1 58.4 %reduce-scatter.2.cloned.1.call-done = bf16[144,8192]{1,0:T(8,128)(2,1)} async-done(((bf16[288,8192]{1,0:T(8,128)(2,1)}), bf16[144,8192]{1,0:T(8,128)(2,1)}) %reduce-scatter.2.cloned.1.call-update) | async-done | bytes 2359312 | tf_op jit(solution)/shard_map/reduce_scatter | solution.py:97
  (8 shorter events, 0.0 us)
Async XLA Ops:
  6.5 47.2 %all-gather.10.cloned.1.call-start = ((), (), s32[]{:S(2)}) async-start(), calls=%async_computation.2 | async-start | bytes 2228224 | tf_op jit(solution)/shard_map/all_gather | solution.py:39
  7.3 88.8 %all-gather.12.cloned.1.call-start = ((), (), s32[]{:S(2)}) async-start(), calls=%async_computation.3 | async-start | bytes 2228224 | tf_op jit(solution)/shard_map/all_gather | solution.py:43
  8.0 163.3 %all-gather.8.cloned.1.call-start = ((), (), s32[]{:S(2)}) async-start(), calls=%async_computation.1 | async-start | bytes 8912896 | tf_op jit(solution)/shard_map/all_gather | solution.py:35
  8.7 201.6 %all-gather.18.cloned.1.call-start = ((), (), s32[]{:S(2)}) async-start(), calls=%async_computation.7 | async-start | bytes 1253376 | tf_op jit(solution)/shard_map/all_gather | solution.py:63
  13.5 46.2 %copy-start.1 = (bf16[128]{0:T(256)(128)(2,1)S(1)}, bf16[128]{0:T(256)(128)(2,1)}, u32[]{:S(2)}) copy-start(bf16[128]{0:T(256)(128)(2,1)} %param.18) | copy-start | bytes 772
  58.3 43.8 %copy-start = (bf16[512]{0:T(512)(128)(2,1)S(1)}, bf16[512]{0:T(512)(128)(2,1)}, u32[]{:S(2)}) copy-start(bf16[512]{0:T(512)(128)(2,1)} %param.16) | copy-start | bytes 3076
  59.7 190.0 %all-gather.14.cloned.1.call-start = ((), (), s32[]{:S(2)}) async-start(), calls=%async_computation.4 | async-start | bytes 1253376 | tf_op jit(solution)/shard_map/all_gather | solution.py:64
  101.2 227.1 %all-gather.16.cloned.1.call-start = ((), (), s32[]{:S(2)}) async-start(), calls=%async_computation.5 | async-start | bytes 8912896 | tf_op jit(solution)/shard_map/all_gather | solution.py:94
  101.8 292.6 %reduce-scatter.2.cloned.1.call-start = ((), (), s32[]{:S(2)}) async-start(), calls=%async_computation.6 | async-start | bytes 7077888 | tf_op jit(solution)/shard_map/reduce_scatter | solution.py:97
Sparse Core Ops, SparseCore 0:
  9.5 44.1 all-gather.9
  55.9 40.1 all-gather.11
  98.2 73.0 all-gather.7
  173.4 36.8 all-gather.17
  212.5 37.1 all-gather.13
  251.7 76.5 all-gather.15
  336.2 58.2 reduce-scatter.1
where the time goes:
time: 402 us; the launch traced here: 401 us
  waiting for transfers between devices  336 us (84%)
  matrix products  36.6 us (9%)
  other arithmetic  14.4 us (4%)
  between operations  13.6 us (3%)
    all_gather x1, waiting for transfers between devices, local(): lax.all_gather(w_query, 'seq', axis=0, tiled=True)  68.6 us
    all_gather x1, waiting for transfers between devices, local(): lax.all_gather(w_out, 'seq', axis=1, tiled=True)  59.2 us
    reduce_scatter x1, waiting for transfers between devices, local(): lax.psum_scatter(partial_out.astype(jnp.bfloat16), 'head', scatter_dimens...  58.4 us
    all_gather x1, waiting for transfers between devices, local(): lax.all_gather(w_key, 'seq', axis=0, tiled=True)  40.1 us
    all_gather x1, waiting for transfers between devices, local(): value_piece = lax.all_gather(values, 'seq', axis=0, tiled=True)  39.3 us
    all_gather x1, waiting for transfers between devices, local(): lax.all_gather(w_value, 'seq', axis=0, tiled=True)  36.3 us
    all_gather x1, waiting for transfers between devices, local(): key_piece = lax.all_gather(keys, 'seq', axis=0, tiled=True)  31.1 us
  transfers between devices with their start and end apart: 7, of which 7 were waited for; matrix products, arithmetic and copies ran while one was open for 11% of the time, Pallas kernels for 0%

commit v1 on v0

--- a/solution.py
+++ b/solution.py
@@ -6,6 +6,18 @@
 HEAD_DIM = 128
 ROPE_BASE = 1000000.0
 EPSILON = 1e-06
+
+
+def collect(value, axis, dim):
+    ways, here, step = (lax.axis_size(axis), lax.axis_index(axis), value.shape[dim])
+    shape = [n * ways if d == dim else n for d, n in enumerate(value.shape)]
+    full = lax.dynamic_update_slice_in_dim(
+        jnp.zeros(shape, value.dtype), value, here * step, axis=dim
+    )
+    for far in range(1, ways):
+        value = lax.ppermute(value, axis, [(d, (d + 1) % ways) for d in range(ways)])
+        full = lax.dynamic_update_slice_in_dim(full, value, (here - far) % ways * step, axis=dim)
+    return full
 
 
 def rotary(values, positions):
@@ -35,9 +47,7 @@
         lax.all_gather(w_query, "seq", axis=0, tiled=True),
         preferred_element_type=jnp.float32,
     )
-    keys = jnp.dot(
-        normed, lax.all_gather(w_key, "seq", axis=0, tiled=True), preferred_element_type=jnp.float32
-    )
+    keys = jnp.dot(normed, collect(w_key, "seq", 0), preferred_element_type=jnp.float32)
     values = jnp.dot(
         normed,
         lax.all_gather(w_value, "seq", axis=0, tiled=True),

time: 402 us -> 370 us (0.920)
  waiting for transfers between devices: 336 us -> 306 us
    ppermute x0 -> x15, waiting for transfers between devices: none -> 121 us  [collect(): lax.ppermute(value, axis, [(d, (d + 1) % ways) for d in range(ways)])]
    all_gather x1, waiting for transfers between devices: 68.6 us -> 0.02 us  [local(): lax.all_gather(w_query, 'seq', axis=0, tiled=True)]
    all_gather x1 -> x0, waiting for transfers between devices: 40.1 us -> none  [local(): lax.all_gather(w_key, 'seq', axis=0, tiled=True)]
    all_gather x1, waiting for transfers between devices: 36.3 us -> 0.02 us  [local(): lax.all_gather(w_value, 'seq', axis=0, tiled=True)]
    all_gather x1, waiting for transfers between devices: 31.1 us -> 25.7 us  [local(): key_piece = lax.all_gather(keys, 'seq', axis=0, tiled=True)]
  transfers between devices with their start and end apart: 7 -> 21, of which waited for: 7 -> 19; matrix products, arithmetic and copies ran while one was open for 11% -> 11% of each run, Pallas kernels for 0% -> 0%
where the time goes in v1:
time: 370 us; the launch traced here: 369 us
  waiting for transfers between devices  306 us (83%)
  matrix products  33.8 us (9%)
  between operations  14.2 us (4%)
  other arithmetic  13 us (4%)
    ppermute x15, waiting for transfers between devices, collect(): lax.ppermute(value, axis, [(d, (d + 1) % ways) for d in range(ways)])  121 us
    all_gather x1, waiting for transfers between devices, local(): lax.all_gather(w_out, 'seq', axis=1, tiled=True)  59.2 us
    reduce_scatter x1, waiting for transfers between devices, local(): lax.psum_scatter(partial_out.astype(jnp.bfloat16), 'head', scatter_dimens...  58.4 us
    all_gather x1, waiting for transfers between devices, local(): value_piece = lax.all_gather(values, 'seq', axis=0, tiled=True)  39.3 us
    all_gather x1, waiting for transfers between devices, local(): key_piece = lax.all_gather(keys, 'seq', axis=0, tiled=True)  25.7 us
    dot_general x1, matrix products, local(): jnp.dot(attended, lax.all_gather(w_out, 'seq', axis=1, tiled=True), prefe...  7.84 us
  transfers between devices with their start and end apart: 21, of which 19 were waited for; matrix products, arithmetic and copies ran while one was open for 11% of the time, Pallas kernels for 0%

profile of v1, /device:TPU:0, one launch (start us, length us, event | category | flops | bytes accessed | tf_op | source)
XLA Modules:
  0.0 369.3 jit_solution(14243874097703184129)
XLA Ops:
  6.5 0.7 all-gather.9.cloned.1.call-update
  7.3 0.0 all-gather.7.cloned.1.call-start
  7.3 0.7 all-gather.7.cloned.1.call-update
  8.0 0.0 all-gather.15.cloned.1.call-start
  8.1 0.5 collective-permute-start
  8.6 7.8 %collective-permute-done = bf16[512,128]{1,0:T(8,128)(2,1)S(1)} collective-permute-done((bf16[512,128]{1,0:T(8,128)(2,1)}, bf16[512,128]{1,0:T(8,128)(2,1)S(1)}, u32[]{:S(2)}, u32[]{:S(2)}) %collective-permute-start) | collective-permute-done | bytes 131104 | tf_op jit(solution)/shard_map/ppermute | solution.py:18
  16.4 0.0 collective-permute-start.1
  16.4 7.2 %collective-permute-done.1 = bf16[512,128]{1,0:T(8,128)(2,1)S(1)} collective-permute-done((bf16[512,128]{1,0:T(8,128)(2,1)S(1)}, bf16[512,128]{1,0:T(8,128)(2,1)S(1)}, u32[]{:S(2)}, u32[]{:S(2)}) %collective-permute-start.1) | collective-permute-done | bytes 131104 | tf_op jit(solution)/shard_map/ppermute | solution.py:18
  23.6 0.0 collective-permute-start.2
  23.6 8.6 %collective-permute-done.2 = bf16[512,128]{1,0:T(8,128)(2,1)S(1)} collective-permute-done((bf16[512,128]{1,0:T(8,128)(2,1)S(1)}, bf16[512,128]{1,0:T(8,128)(2,1)S(1)}, u32[]{:S(2)}, u32[]{:S(2)}) %collective-permute-start.2) | collective-permute-done | bytes 131104 | tf_op jit(solution)/shard_map/ppermute | solution.py:18
  32.2 0.0 collective-permute-start.3
  32.2 7.1 %collective-permute-done.3 = bf16[512,128]{1,0:T(8,128)(2,1)S(1)} collective-permute-done((bf16[512,128]{1,0:T(8,128)(2,1)S(1)}, bf16[512,128]{1,0:T(8,128)(2,1)S(1)}, u32[]{:S(2)}, u32[]{:S(2)}) %collective-permute-start.3) | collective-permute-done | bytes 131104 | tf_op jit(solution)/shard_map/ppermute | solution.py:18
  39.3 0.0 collective-permute-start.4
  39.3 8.9 %collective-permute-done.4 = bf16[512,128]{1,0:T(8,128)(2,1)S(1)} collective-permute-done((bf16[512,128]{1,0:T(8,128)(2,1)S(1)}, bf16[512,128]{1,0:T(8,128)(2,1)S(1)}, u32[]{:S(2)}, u32[]{:S(2)}) %collective-permute-start.4) | collective-permute-done | bytes 131104 | tf_op jit(solution)/shard_map/ppermute | solution.py:18
  48.2 0.0 collective-permute-start.5
  48.2 3.4 fusion.11
  51.5 3.8 %collective-permute-done.5 = bf16[512,128]{1,0:T(8,128)(2,1)S(1)} collective-permute-done((bf16[512,128]{1,0:T(8,128)(2,1)S(1)}, bf16[512,128]{1,0:T(8,128)(2,1)S(1)}, u32[]{:S(2)}, u32[]{:S(2)}) %collective-permute-start.5) | collective-permute-done | bytes 131104 | tf_op jit(solution)/shard_map/ppermute | solution.py:18
  55.3 0.0 collective-permute-start.6
  55.3 7.1 %collective-permute-done.6 = bf16[512,128]{1,0:T(8,128)(2,1)S(1)} collective-permute-done((bf16[512,128]{1,0:T(8,128)(2,1)S(1)}, bf16[512,128]{1,0:T(8,128)(2,1)S(1)}, u32[]{:S(2)}, u32[]{:S(2)}) %collective-permute-start.6) | collective-permute-done | bytes 131104 | tf_op jit(solution)/shard_map/ppermute | solution.py:18
  62.4 0.0 collective-permute-start.7
  62.9 0.0 copy-start
  62.9 0.3 broadcast_in_dim.18
  63.2 6.4 %collective-permute-done.7 = bf16[512,128]{1,0:T(8,128)(2,1)S(1)} collective-permute-done((bf16[512,128]{1,0:T(8,128)(2,1)S(1)}, bf16[512,128]{1,0:T(8,128)(2,1)S(1)}, u32[]{:S(2)}, u32[]{:S(2)}) %collective-permute-start.7) | collective-permute-done | bytes 131104 | tf_op jit(solution)/shard_map/ppermute | solution.py:18
  69.6 0.0 collective-permute-start.8
  69.7 10.0 %collective-permute-done.8 = bf16[512,128]{1,0:T(8,128)(2,1)S(1)} collective-permute-done((bf16[512,128]{1,0:T(8,128)(2,1)S(1)}, bf16[512,128]{1,0:T(8,128)(2,1)S(1)}, u32[]{:S(2)}, u32[]{:S(2)}) %collective-permute-start.8) | collective-permute-done | bytes 131104 | tf_op jit(solution)/shard_map/ppermute | solution.py:18
  79.7 9.9 %collective-permute-done.9 = bf16[512,128]{1,0:T(8,128)(2,1)S(1)} collective-permute-done((bf16[512,128]{1,0:T(8,128)(2,1)S(1)}, bf16[512,128]{1,0:T(8,128)(2,1)S(1)}, u32[]{:S(2)}, u32[]{:S(2)}) %collective-permute-start.9) | collective-permute-done | bytes 131104 | tf_op jit(solution)/shard_map/ppermute | solution.py:18
  89.7 7.1 %collective-permute-done.10 = bf16[512,128]{1,0:T(8,128)(2,1)S(1)} collective-permute-done((bf16[512,128]{1,0:T(8,128)(2,1)S(1)}, bf16[512,128]{1,0:T(8,128)(2,1)S(1)}, u32[]{:S(2)}, u32[]{:S(2)}) %collective-permute-start.10) | collective-permute-done | bytes 131104 | tf_op jit(solution)/shard_map/ppermute | solution.py:18
  96.9 10.0 %collective-permute-done.11 = bf16[512,128]{1,0:T(8,128)(2,1)S(1)} collective-permute-done((bf16[512,128]{1,0:T(8,128)(2,1)S(1)}, bf16[512,128]{1,0:T(8,128)(2,1)S(1)}, u32[]{:S(2)}, u32[]{:S(2)}) %collective-permute-start.11) | collective-permute-done | bytes 131104 | tf_op jit(solution)/shard_map/ppermute | solution.py:18
  106.9 10.0 %collective-permute-done.12 = bf16[512,128]{1,0:T(8,128)(2,1)S(1)} collective-permute-done((bf16[512,128]{1,0:T(8,128)(2,1)S(1)}, bf16[512,128]{1,0:T(8,128)(2,1)S(1)}, u32[]{:S(2)}, u32[]{:S(2)}) %collective-permute-start.12) | collective-permute-done | bytes 131104 | tf_op jit(solution)/shard_map/ppermute | solution.py:18
  116.9 0.0 collective-permute-start.13
  116.9 7.6 %collective-permute-done.13 = bf16[512,128]{1,0:T(8,128)(2,1)S(1)} collective-permute-done((bf16[512,128]{1,0:T(8,128)(2,1)S(1)}, bf16[512,128]{1,0:T(8,128)(2,1)S(1)}, u32[]{:S(2)}, u32[]{:S(2)}) %collective-permute-start.13) | collective-permute-done | bytes 131104 | tf_op jit(solution)/shard_map/ppermute | solution.py:18
  124.5 0.0 collective-permute-start.14
  124.6 10.0 %collective-permute-done.14 = bf16[512,128]{1,0:T(8,128)(2,1)S(1)} collective-permute-done((bf16[512,128]{1,0:T(8,128)(2,1)S(1)}, bf16[512,128]{1,0:T(8,128)(2,1)S(1)}, u32[]{:S(2)}, u32[]{:S(2)}) %collective-permute-start.14) | collective-permute-done | bytes 131104 | tf_op jit(solution)/shard_map/ppermute | solution.py:18
  134.6 0.0 copy-start.5
  134.6 1.6 fusion.14
  136.3 0.6 fusion.24
  136.9 0.7 pad_maximum_fusion
  137.7 0.0 all-gather.15.cloned.1.call-update
  137.7 0.0 all-gather.11.cloned.1.call-start
  137.8 0.0 copy-start.3
  137.8 0.0 all-gather.9.cloned.1.call-done
  137.8 5.2 %fusion.15 = bf16[288,128]{1,0:T(8,128)(2,1)} fusion(bf16[8192,128]{1,0:T(8,128)(2,1)} %all-gather.9.cloned.1.call-done, f32[128]{0:T(128)S(1)} %convert_element_type.54, bf16[288,8192]{1,0:T(8,128)(2,1)} %param.11, f32[8192]{0:T(1024)S(1)} %convert_element_type.48, f32[288]{0:T(512)S(1)} %add_rsqrt_fusion), kind=kOutput, calls=%fused_computation.25 | convolution fusion | flops 613490688 | bytes 6923904 | tf_op jit(solution)/shard_map/dot_general | solution.py:51
  143.0 0.0 all-gather.11.cloned.1.call-update
  143.0 0.0 all-gather.13.cloned.1.call-start
  143.0 0.5 all-gather.13.cloned.1.call-update
  143.6 0.2 reduce-scatter.2.cloned.1.call-start
  143.8 0.6 multiply_cosine_fusion.1
  144.4 0.0 all-gather.7.cloned.1.call-done
  144.5 7.1 %convolution_add_fusion = f32[288,512]{1,0:T(8,128)S(1)} fusion(bf16[8192,512]{1,0:T(8,128)(2,1)} %all-gather.7.cloned.1.call-done, f32[512]{0:T(512)S(1)} %convert_element_type.50, bf16[288,8192]{1,0:T(8,128)(2,1)} %param.11, f32[8192]{0:T(1024)S(1)} %convert_element_type.48, f32[288]{0:T(512)S(1)} %add_rsqrt_fusion), kind=kOutput, calls=%fused_computation.21 | convolution fusion | flops 2425503744 | bytes 13732992 | tf_op jit(solution)/shard_map/dot_general | solution.py:45
  151.6 0.2 reshape.159
  151.8 0.4 fusion.30
  152.2 0.2 subtract_convert_fusion
  152.3 0.2 maximum_bitcast_fusion
  152.5 25.7 %all-gather.15.cloned.1.call-done = bf16[4608,1,128]{2,0,1:T(8,128)(2,1)} async-done(((bf16[288,1,128]{2,0,1:T(8,128)(2,1)}), bf16[4608,1,128]{2,0,1:T(8,128)(2,1)}) %all-gather.15.cloned.1.call-update) | async-done | bytes 1179664 | tf_op jit(solution)/shard_map/all_gather | solution.py:73
  178.2 39.3 %all-gather.11.cloned.1.call-done = bf16[4608,128]{1,0:T(8,128)(2,1)} async-done(((bf16[288,128]{1,0:T(8,128)(2,1)}), bf16[4608,128]{1,0:T(8,128)(2,1)}) %all-gather.11.cloned.1.call-update) | async-done | bytes 1179664 | tf_op jit(solution)/shard_map/all_gather | solution.py:74
  217.6 19.4 %conditional.1 = (f32[4,288]{1,0:T(4,128)S(1)}, f32[4,288,128]{2,1,0:T(8,128)S(1)}) conditional(s32[]{:T(128)} %convert_element_type.46, () %tuple.13, (s32[]{:T(128)}, s32[288]{0:T(512)S(1)}, bf16[4,288,128]{2,1,0:T(8,128)(2,1)S(1)}, bf16[4608,128]{1,0:T(8,128)(2,1)}, bf16[4608,128]{1,0:T(8,128)(2,1)}) %tuple.34), branch_computations={%region_1.2_spmd, %region_2.5_spmd} | conditional | flops 2777627648 | bytes 72284560 | solution.py:99
  217.6 0.8 iota_compare_fusion
  218.4 5.4 %fusion = (f32[4,288]{1,0:T(4,128)S(1)}, f32[4,288,4608]{2,1,0:T(8,128)S(1)}) fusion(pred[288,4608]{1,0:T(8,128)(4,1)S(1)} %iota_compare_fusion, bf16[4,288,128]{2,1,0:T(8,128)(2,1)S(1)} %get-tuple-element.19, bf16[4608,128]{1,0:T(8,128)(2,1)} %get-tuple-element.20), kind=kOutput, calls=%fused_computation.2 | convolution fusion | flops 1374878592 | bytes 24039936 | tf_op jit(solution)/shard_map/cond/branch_1_fun/hqd,kd->hqk/dot_general | solution.py:79
  223.8 6.6 %fusion.3 = f32[4,288,128]{2,1,0:T(8,128)S(1)} fusion(f32[4,288,4608]{2,1,0:T(8,128)S(1)} %get-tuple-element.27, f32[4,288]{1,0:T(4,128)S(1)} %broadcast_maximum_fusion, pred[288,4608]{1,0:T(8,128)(4,1)S(1)} %iota_compare_fusion, bf16[4608,128]{1,0:T(8,128)(2,1)} %get-tuple-element.21), kind=kOutput, calls=%fused_computation.5 | convolution fusion | flops 1380188160 | bytes 24334848 | tf_op jit(solution)/shard_map/cond/branch_1_fun/hqk,kd->hqd/dot_general | solution.py:88
  230.4 6.6 %fusion.2 = f32[4,288]{1,0:T(4,128)S(1)} fusion(f32[4,288,4608]{2,1,0:T(8,128)S(1)} %get-tuple-element.27, f32[4,288]{1,0:T(4,128)S(1)} %broadcast_maximum_fusion, pred[288,4608]{1,0:T(8,128)(4,1)S(1)} %iota_compare_fusion), kind=kLoop, calls=%fused_computation.4 | loop fusion | flops 21232512 | bytes 22569984 | tf_op jit(solution)/shard_map/cond/branch_1_fun/reduce_sum | solution.py:87
  237.0 59.2 %all-gather.13.cloned.1.call-done = bf16[512,8192]{1,0:T(8,128)(2,1)} async-done(((bf16[512,512]{1,0:T(8,128)(2,1)}), bf16[512,8192]{1,0:T(8,128)(2,1)}) %all-gather.13.cloned.1.call-update) | async-done | bytes 8388624 | tf_op jit(solution)/shard_map/all_gather | solution.py:104
  296.2 7.8 %convolution_convert_fusion = bf16[288,8192]{1,0:T(8,128)(2,1)} fusion(bf16[512,8192]{1,0:T(8,128)(2,1)} %all-gather.13.cloned.1.call-done, f32[4,288,128]{2,1,0:T(8,128)S(1)} %get-tuple-element.24, f32[4,288]{1,0:T(4,128)S(1)} %get-tuple-element.25), kind=kOutput, calls=%fused_computation.17 | convolution fusion | flops 2418573312 | bytes 13701632 | tf_op jit(solution)/shard_map/dot_general | solution.py:102
  304.1 0.0 reduce-scatter.2.cloned.1.call-update
  304.1 58.4 %reduce-scatter.2.cloned.1.call-done = bf16[144,8192]{1,0:T(8,128)(2,1)} async-done(((bf16[288,8192]{1,0:T(8,128)(2,1)}), bf16[144,8192]{1,0:T(8,128)(2,1)}) %reduce-scatter.2.cloned.1.call-update) | async-done | bytes 2359312 | tf_op jit(solution)/shard_map/reduce_scatter | solution.py:107
  (40 shorter events, 0.4 us)
Async XLA Ops:
  6.5 56.6 %copy-start.1 = (bf16[512,128]{1,0:T(8,128)(2,1)S(1)}, bf16[512,128]{1,0:T(8,128)(2,1)}, u32[]{:S(2)}) copy-start(bf16[512,128]{1,0:T(8,128)(2,1)} %param.14) | copy-start | bytes 393220
  6.5 56.2 %copy-start.2 = (bf16[8192]{0:T(1024)(128)(2,1)S(1)}, bf16[8192]{0:T(1024)(128)(2,1)}, u32[]{:S(2)}) copy-start(bf16[8192]{0:T(1024)(128)(2,1)} %param.12) | copy-start | bytes 49156
  6.5 56.2 %copy-start.4 = (bf16[128]{0:T(256)(128)(2,1)S(1)}, bf16[128]{0:T(256)(128)(2,1)}, u32[]{:S(2)}) copy-start(bf16[128]{0:T(256)(128)(2,1)} %param.17) | copy-start | bytes 772
  6.5 131.3 %all-gather.9.cloned.1.call-start = ((), (), s32[]{:S(2)}) async-start(), calls=%async_computation.2 | async-start | bytes 2228224 | tf_op jit(solution)/shard_map/all_gather | solution.py:53
  7.3 137.2 %all-gather.7.cloned.1.call-start = ((), (), s32[]{:S(2)}) async-start(), calls=%async_computation.1 | async-start | bytes 8912896 | tf_op jit(solution)/shard_map/all_gather | solution.py:47
  8.0 170.2 %all-gather.15.cloned.1.call-start = ((), (), s32[]{:S(2)}) async-start(), calls=%async_computation.6 | async-start | bytes 1253376 | tf_op jit(solution)/shard_map/all_gather | solution.py:73
  8.1 8.4 %collective-permute-start = (bf16[512,128]{1,0:T(8,128)(2,1)}, bf16[512,128]{1,0:T(8,128)(2,1)S(1)}, u32[]{:S(2)}, u32[]{:S(2)}) collective-permute-start(bf16[512,128]{1,0:T(8,128)(2,1)} %param.14), channel_id=1, source_target_pairs={{0,2},{2,4},{4,6},{6,8},{8,10},{10,12},{12,14},{14,16},{16,18},{18... | collective-permute-start | bytes 393224 | tf_op jit(solution)/shard_map/ppermute | solution.py:18
  16.4 7.2 %collective-permute-start.1 = (bf16[512,128]{1,0:T(8,128)(2,1)S(1)}, bf16[512,128]{1,0:T(8,128)(2,1)S(1)}, u32[]{:S(2)}, u32[]{:S(2)}) collective-permute-start(bf16[512,128]{1,0:T(8,128)(2,1)S(1)} %collective-permute-done), channel_id=1, source_target_pairs={{0,2},{2,4},{4,6},{6,8},{8,10},{10,12},{12,14},{14,16},{16,18},{18... | collective-permute-start | bytes 393224 | tf_op jit(solution)/shard_map/ppermute | solution.py:18
  23.6 8.6 %collective-permute-start.2 = (bf16[512,128]{1,0:T(8,128)(2,1)S(1)}, bf16[512,128]{1,0:T(8,128)(2,1)S(1)}, u32[]{:S(2)}, u32[]{:S(2)}) collective-permute-start(bf16[512,128]{1,0:T(8,128)(2,1)S(1)} %collective-permute-done.1), channel_id=1, source_target_pairs={{0,2},{2,4},{4,6},{6,8},{8,10},{10,12},{12,14},{14,16},{16,18},{18... | collective-permute-start | bytes 393224 | tf_op jit(solution)/shard_map/ppermute | solution.py:18
  32.2 7.1 %collective-permute-start.3 = (bf16[512,128]{1,0:T(8,128)(2,1)S(1)}, bf16[512,128]{1,0:T(8,128)(2,1)S(1)}, u32[]{:S(2)}, u32[]{:S(2)}) collective-permute-start(bf16[512,128]{1,0:T(8,128)(2,1)S(1)} %collective-permute-done.2), channel_id=1, source_target_pairs={{0,2},{2,4},{4,6},{6,8},{8,10},{10,12},{12,14},{14,16},{16,18},{18... | collective-permute-start | bytes 393224 | tf_op jit(solution)/shard_map/ppermute | solution.py:18
  39.3 8.9 %collective-permute-start.4 = (bf16[512,128]{1,0:T(8,128)(2,1)S(1)}, bf16[512,128]{1,0:T(8,128)(2,1)S(1)}, u32[]{:S(2)}, u32[]{:S(2)}) collective-permute-start(bf16[512,128]{1,0:T(8,128)(2,1)S(1)} %collective-permute-done.3), channel_id=1, source_target_pairs={{0,2},{2,4},{4,6},{6,8},{8,10},{10,12},{12,14},{14,16},{16,18},{18... | collective-permute-start | bytes 393224 | tf_op jit(solution)/shard_map/ppermute | solution.py:18
  48.2 7.2 %collective-permute-start.5 = (bf16[512,128]{1,0:T(8,128)(2,1)S(1)}, bf16[512,128]{1,0:T(8,128)(2,1)S(1)}, u32[]{:S(2)}, u32[]{:S(2)}) collective-permute-start(bf16[512,128]{1,0:T(8,128)(2,1)S(1)} %collective-permute-done.4), channel_id=1, source_target_pairs={{0,2},{2,4},{4,6},{6,8},{8,10},{10,12},{12,14},{14,16},{16,18},{18... | collective-permute-start | bytes 393224 | tf_op jit(solution)/shard_map/ppermute | solution.py:18
  55.3 7.1 %collective-permute-start.6 = (bf16[512,128]{1,0:T(8,128)(2,1)S(1)}, bf16[512,128]{1,0:T(8,128)(2,1)S(1)}, u32[]{:S(2)}, u32[]{:S(2)}) collective-permute-start(bf16[512,128]{1,0:T(8,128)(2,1)S(1)} %collective-permute-done.5), channel_id=1, source_target_pairs={{0,2},{2,4},{4,6},{6,8},{8,10},{10,12},{12,14},{14,16},{16,18},{18... | collective-permute-start | bytes 393224 | tf_op jit(solution)/shard_map/ppermute | solution.py:18
  62.4 7.2 %collective-permute-start.7 = (bf16[512,128]{1,0:T(8,128)(2,1)S(1)}, bf16[512,128]{1,0:T(8,128)(2,1)S(1)}, u32[]{:S(2)}, u32[]{:S(2)}) collective-permute-start(bf16[512,128]{1,0:T(8,128)(2,1)S(1)} %collective-permute-done.6), channel_id=1, source_target_pairs={{0,2},{2,4},{4,6},{6,8},{8,10},{10,12},{12,14},{14,16},{16,18},{18... | collective-permute-start | bytes 393224 | tf_op jit(solution)/shard_map/ppermute | solution.py:18
  62.9 71.7 %copy-start = (bf16[288,8192]{1,0:T(8,128)(2,1)S(1)}, bf16[288,8192]{1,0:T(8,128)(2,1)}, u32[]{:S(2)}) copy-start(bf16[288,8192]{1,0:T(8,128)(2,1)} %param.11) | copy-start | bytes 14155780
  69.6 10.0 %collective-permute-start.8 = (bf16[512,128]{1,0:T(8,128)(2,1)S(1)}, bf16[512,128]{1,0:T(8,128)(2,1)S(1)}, u32[]{:S(2)}, u32[]{:S(2)}) collective-permute-start(bf16[512,128]{1,0:T(8,128)(2,1)S(1)} %collective-permute-done.7), channel_id=1, source_target_pairs={{0,2},{2,4},{4,6},{6,8},{8,10},{10,12},{12,14},{14,16},{16,18},{18... | collective-permute-start | bytes 393224 | tf_op jit(solution)/shard_map/ppermute | solution.py:18
  79.6 10.0 %collective-permute-start.9 = (bf16[512,128]{1,0:T(8,128)(2,1)S(1)}, bf16[512,128]{1,0:T(8,128)(2,1)S(1)}, u32[]{:S(2)}, u32[]{:S(2)}) collective-permute-start(bf16[512,128]{1,0:T(8,128)(2,1)S(1)} %collective-permute-done.8), channel_id=1, source_target_pairs={{0,2},{2,4},{4,6},{6,8},{8,10},{10,12},{12,14},{14,16},{16,18},{18... | collective-permute-start | bytes 393224 | tf_op jit(solution)/shard_map/ppermute | solution.py:18
  89.6 7.2 %collective-permute-start.10 = (bf16[512,128]{1,0:T(8,128)(2,1)S(1)}, bf16[512,128]{1,0:T(8,128)(2,1)S(1)}, u32[]{:S(2)}, u32[]{:S(2)}) collective-permute-start(bf16[512,128]{1,0:T(8,128)(2,1)S(1)} %collective-permute-done.9), channel_id=1, source_target_pairs={{0,2},{2,4},{4,6},{6,8},{8,10},{10,12},{12,14},{14,16},{16,18},{18... | collective-permute-start | bytes 393224 | tf_op jit(solution)/shard_map/ppermute | solution.py:18
  96.8 10.0 %collective-permute-start.11 = (bf16[512,128]{1,0:T(8,128)(2,1)S(1)}, bf16[512,128]{1,0:T(8,128)(2,1)S(1)}, u32[]{:S(2)}, u32[]{:S(2)}) collective-permute-start(bf16[512,128]{1,0:T(8,128)(2,1)S(1)} %collective-permute-done.10), channel_id=1, source_target_pairs={{0,2},{2,4},{4,6},{6,8},{8,10},{10,12},{12,14},{14,16},{16,18},{18... | collective-permute-start | bytes 393224 | tf_op jit(solution)/shard_map/ppermute | solution.py:18
  106.9 10.0 %collective-permute-start.12 = (bf16[512,128]{1,0:T(8,128)(2,1)S(1)}, bf16[512,128]{1,0:T(8,128)(2,1)S(1)}, u32[]{:S(2)}, u32[]{:S(2)}) collective-permute-start(bf16[512,128]{1,0:T(8,128)(2,1)S(1)} %collective-permute-done.11), channel_id=1, source_target_pairs={{0,2},{2,4},{4,6},{6,8},{8,10},{10,12},{12,14},{14,16},{16,18},{18... | collective-permute-start | bytes 393224 | tf_op jit(solution)/shard_map/ppermute | solution.py:18
  116.9 7.6 %collective-permute-start.13 = (bf16[512,128]{1,0:T(8,128)(2,1)S(1)}, bf16[512,128]{1,0:T(8,128)(2,1)S(1)}, u32[]{:S(2)}, u32[]{:S(2)}) collective-permute-start(bf16[512,128]{1,0:T(8,128)(2,1)S(1)} %collective-permute-done.12), channel_id=1, source_target_pairs={{0,2},{2,4},{4,6},{6,8},{8,10},{10,12},{12,14},{14,16},{16,18},{18... | collective-permute-start | bytes 393224 | tf_op jit(solution)/shard_map/ppermute | solution.py:18
  124.5 10.1 %collective-permute-start.14 = (bf16[512,128]{1,0:T(8,128)(2,1)S(1)}, bf16[512,128]{1,0:T(8,128)(2,1)S(1)}, u32[]{:S(2)}, u32[]{:S(2)}) collective-permute-start(bf16[512,128]{1,0:T(8,128)(2,1)S(1)} %collective-permute-done.13), channel_id=1, source_target_pairs={{0,2},{2,4},{4,6},{6,8},{8,10},{10,12},{12,14},{14,16},{16,18},{18... | collective-permute-start | bytes 393224 | tf_op jit(solution)/shard_map/ppermute | solution.py:18
  134.6 3.1 copy-start.5
  137.7 79.9 %all-gather.11.cloned.1.call-start = ((), (), s32[]{:S(2)}) async-start(), calls=%async_computation.3 | async-start | bytes 1253376 | tf_op jit(solution)/shard_map/all_gather | solution.py:74
  137.8 6.1 %copy-start.3 = (bf16[512]{0:T(512)(128)(2,1)S(1)}, bf16[512]{0:T(512)(128)(2,1)}, u32[]{:S(2)}) copy-start(bf16[512]{0:T(512)(128)(2,1)} %param.16) | copy-start | bytes 3076
  143.0 153.2 %all-gather.13.cloned.1.call-start = ((), (), s32[]{:S(2)}) async-start(), calls=%async_computation.4 | async-start | bytes 8912896 | tf_op jit(solution)/shard_map/all_gather | solution.py:104
  143.6 218.9 %reduce-scatter.2.cloned.1.call-start = ((), (), s32[]{:S(2)}) async-start(), calls=%async_computation.5 | async-start | bytes 7077888 | tf_op jit(solution)/shard_map/reduce_scatter | solution.py:107
Sparse Core Ops, SparseCore 0:
  9.5 46.1 all-gather.8
  57.8 78.5 all-gather.6
  138.7 39.5 all-gather.14
  180.4 37.1 all-gather.10
  219.6 76.5 all-gather.12
  304.2 58.2 reduce-scatter.1
